TPU v7x, 32 devices: a whole 2x2x4 slice. The times are simulated.
32 devices in a mesh: row: 4 (over y, core), col: 8 (over z, x).
Axes of the slice: x: 2, y: 2, z: 4, core: 2. Of those that a mesh axis runs over, the one named last changes fastest.
Arguments:
- phase: float32 [512, 32, 512], P('col', 'row'), may hold values from -6 to 6
- velocity: float32 [3, 512, 32, 512], P(None, 'col', 'row'), may hold values from -12 to 12
Outputs:
- phase_next: float32 [512, 32, 512], P('col', 'row')
- velocity_next: float32 [3, 512, 32, 512], P(None, 'col', 'row')
All inputs are finite; a program needn't handle non-finite values.
Results may differ from a plain program's by a relative error of at most 0.013.
Values may be sent and summed in bfloat16 or wider, within the bound.
A program may use at most 128 MiB of HBM per device.

v0:
```python
import math
import jax
import jax.numpy as jnp
from jax import lax
from jax.sharding import PartitionSpec as P

NX = 512
NY = 512
KC = 192
KY = 384
time_step = 0.001
epsilon = 0.01
mobility = 1.0
reynolds = 100.0
stabilizer = 2.0


def cos_sin(row_index, col_index, period):
    residue = row_index[:, None] * col_index[None, :] % period
    angles = residue.astype(jnp.float32) * (2.0 * math.pi / period)
    return jnp.stack([jnp.cos(angles), jnp.sin(angles)]).astype(jnp.bfloat16)


def pair_sum(pieces, direction, stack_axis):
    if direction < 0:
        real_part = pieces[0, 0] + pieces[1, 1]
        imag_part = pieces[1, 0] - pieces[0, 1]
    else:
        real_part = pieces[0, 0] - pieces[1, 1]
        imag_part = pieces[0, 1] + pieces[1, 0]
    return jnp.stack([real_part, imag_part], axis=stack_axis)


def times_i(values):
    return jnp.stack([-values[:, 1], values[:, 0]], axis=1)


def phase_terms(phase, velocity, gradient, lap_field):
    advect = velocity[0] * gradient[0] + velocity[1] * gradient[1] + velocity[2] * gradient[2]
    bulk_term = phase * phase * phase - phase
    potential = bulk_term - epsilon * epsilon * lap_field
    return (advect, bulk_term, potential)


def momentum(velocity, vortex, gradient, potential):
    return jnp.stack(
        [
            velocity[1] * vortex[2] - velocity[2] * vortex[1] + potential * gradient[0],
            velocity[2] * vortex[0] - velocity[0] * vortex[2] + potential * gradient[1],
            velocity[0] * vortex[1] - velocity[1] * vortex[0] + potential * gradient[2],
        ]
    )


def on_device(phase, velocity):
    col_count = lax.axis_size("col")
    row_count = lax.axis_size("row")
    rows_y = phase.shape[0]
    planes = phase.shape[1]
    total_z = planes * row_count
    half_z = 3 * total_z // 8
    modes_z = 2 * half_z
    kx_local = KC // col_count
    ky_local = KY // row_count
    scale_inv = 1.0 / (NX * NY * total_z)
    table_x = cos_sin(jnp.arange(NX, dtype=jnp.int32), jnp.arange(KC, dtype=jnp.int32), NX)
    table_y = cos_sin(jnp.arange(NY, dtype=jnp.int32), jnp.arange(KY, dtype=jnp.int32) - KC, NY)
    table_z = cos_sin(
        jnp.arange(total_z, dtype=jnp.int32), jnp.arange(modes_z, dtype=jnp.int32) - half_z, total_z
    )
    y_forward = table_y.reshape(2, col_count, rows_y, KY)
    y_inverse = table_y.reshape(2, col_count, rows_y, row_count, ky_local)
    z_table = table_z.reshape(2, row_count, planes, modes_z)
    weight = jnp.where(jnp.arange(KC) == 0, 1.0, 2.0).astype(jnp.bfloat16)[:, None, None, None]

    def along_y(incoming):
        field_count = incoming.shape[1]
        shaped = incoming.reshape(incoming.shape[0], field_count, col_count, 2, rows_y, planes)
        pieces = jnp.einsum(
            "afcpyz,tcyb->ptafbz", shaped, y_forward, preferred_element_type=jnp.float32
        )
        joined = pair_sum(pieces, -1, 2).astype(jnp.bfloat16)
        return joined.reshape(incoming.shape[0], field_count, 2, KY * planes)

    def along_z(incoming):
        field_count = incoming.shape[1]
        shaped = incoming.reshape(incoming.shape[0], field_count, 2, row_count, ky_local, planes)
        pieces = jnp.einsum(
            "afprbz,trzm->ptafbm", shaped, z_table, preferred_element_type=jnp.float32
        )
        joined = pair_sum(pieces, -1, 2) * scale_inv
        return joined.reshape(incoming.shape[0], field_count, 2, ky_local * modes_z)

    def back_y(incoming):
        field_count = incoming.shape[1]
        shaped = incoming.reshape(incoming.shape[0], field_count, 2, row_count, planes, ky_local)
        pieces = jnp.einsum(
            "afprzb,tcyrb->ptafcyz", shaped, y_inverse, preferred_element_type=jnp.float32
        )
        joined = pair_sum(pieces, 1, 3).astype(jnp.bfloat16)
        return joined.reshape(incoming.shape[0], field_count, col_count * 2 * rows_y * planes)

    def back_x(incoming):
        field_count = incoming.shape[1]
        shaped = incoming.reshape(KC, field_count, 2, rows_y, planes)
        scaled = jnp.stack([shaped[:, :, 0] * weight, -(shaped[:, :, 1] * weight)], axis=2)
        return jnp.einsum("afpyz,pxa->fyzx", scaled, table_x, preferred_element_type=jnp.float32)

    def forward(fields):
        field_count = fields.shape[0]
        pieces = jnp.einsum(
            "fyzx,txa->tafyz",
            fields.astype(jnp.bfloat16),
            table_x,
            preferred_element_type=jnp.float32,
        )
        x_lines = jnp.stack([pieces[0], -pieces[1]], axis=2).astype(jnp.bfloat16)
        x_lines = x_lines.reshape(KC, field_count, 2 * rows_y * planes)
        spread = along_y(lax.all_to_all(x_lines, "col", split_axis=0, concat_axis=2, tiled=True))
        return along_z(lax.all_to_all(spread, "row", split_axis=3, concat_axis=3, tiled=True))

    def inverse(spectra):
        field_count = spectra.shape[1]
        shaped = spectra.astype(jnp.bfloat16).reshape(kx_local, field_count, 2, ky_local, modes_z)
        pieces = jnp.einsum(
            "afpbm,trzm->ptafrzb", shaped, z_table, preferred_element_type=jnp.float32
        )
        z_planes = (
            pair_sum(pieces, 1, 2)
            .astype(jnp.bfloat16)
            .reshape(kx_local, field_count, 2, total_z * ky_local)
        )
        spread = back_y(lax.all_to_all(z_planes, "row", split_axis=3, concat_axis=3, tiled=True))
        return back_x(lax.all_to_all(spread, "col", split_axis=2, concat_axis=0, tiled=True))

    spectra = forward(jnp.concatenate([phase[None], velocity], axis=0))
    wave_x = (lax.axis_index("col") * kx_local + jnp.arange(kx_local, dtype=jnp.int32)).astype(
        jnp.float32
    )[:, None, None]
    modes_y = lax.axis_index("row") * ky_local + jnp.arange(ky_local, dtype=jnp.int32) - KC
    wave_y = jnp.broadcast_to(modes_y.astype(jnp.float32)[:, None], (ky_local, modes_z)).reshape(-1)
    z_values = (jnp.arange(modes_z, dtype=jnp.int32) - half_z).astype(jnp.float32) * (NX / total_z)
    wave_z = jnp.broadcast_to(z_values[None, :], (ky_local, modes_z)).reshape(-1)
    squared = wave_x * wave_x + wave_y * wave_y + wave_z * wave_z
    coeff_phase = spectra[:, 0]
    coeff_u = spectra[:, 1]
    coeff_v = spectra[:, 2]
    coeff_w = spectra[:, 3]
    gradients = [
        times_i(wave_x * coeff_phase),
        times_i(wave_y * coeff_phase),
        times_i(wave_z * coeff_phase),
    ]
    laplace = -squared * coeff_phase
    vortex_hat = [
        times_i(wave_y * coeff_w - wave_z * coeff_v),
        times_i(wave_z * coeff_u - wave_x * coeff_w),
        times_i(wave_x * coeff_v - wave_y * coeff_u),
    ]
    leading = inverse(jnp.stack(gradients + [laplace], axis=1))
    advect, bulk_term, potential = phase_terms(phase, velocity, leading[0:3], leading[3])
    phase_side = forward(jnp.stack([advect, bulk_term]))
    vortex = inverse(jnp.stack(vortex_hat, axis=1))
    flow_side = forward(momentum(velocity, vortex, leading[0:3], potential))
    nonlinear = jnp.concatenate([phase_side, flow_side], axis=1)
    mean_mode = (wave_x == 0) & (wave_y == 0) & (wave_z == 0)
    advect_hat = jnp.where(mean_mode, 0.0, nonlinear[:, 0])
    bulk_hat = nonlinear[:, 1]
    stable_part = 1.0 / time_step + mobility * stabilizer * squared
    new_phase = (stable_part * coeff_phase - advect_hat - mobility * squared * bulk_hat) / (
        stable_part + mobility * epsilon * epsilon * squared * squared
    )
    viscous = 1.0 / time_step + squared / reynolds
    unprojected = [
        (spectra[:, 1 + j] / time_step + nonlinear[:, 2 + j]) / viscous for j in range(3)
    ]
    normal_part = (
        wave_x * unprojected[0] + wave_y * unprojected[1] + wave_z * unprojected[2]
    ) / jnp.maximum(squared, 1.0)
    waves = [wave_x, wave_y, wave_z]
    new_flow = [unprojected[j] - waves[j] * normal_part for j in range(3)]
    result = inverse(jnp.stack([new_phase] + new_flow, axis=1))
    return (result[0], result[1:4])


def solution(mesh):
    return jax.shard_map(
        on_device,
        mesh=mesh,
        in_specs=(P("col", "row", None), P(None, "col", "row", None)),
        out_specs=(P("col", "row", None), P(None, "col", "row", None)),
        check_vma=False,
    )
```

profile of v0, /device:TPU:0, one launch (start us, length us, event | category | flops | bytes accessed | tf_op | source)
XLA Modules:
  0.0 845.1 jit_solution(9600123166907076406)
XLA Ops:
  31.2 26.8 %all-to-all-done = bf16[192,4,1024]{2,1,0:T(4,128)(2,1)S(1)} async-done(((bf16[192,4,1024]{2,1,0:T(4,128)(2,1)}), bf16[192,4,1024]{2,1,0:T(4,128)(2,1)S(1)}, u32[]{:S(2)}, u32[]{:S(2)}) %all-to-all-start) | async-done | bytes 1572896 | tf_op jit(solution)/shard_map/all_to_all | solution.py:119
  87.2 25.2 %copy.564 = bf16[24,4,2,3072]{0,1,2,3:T(4,128)(2,1)} copy(bf16[24,4,2,3072]{0,3,1,2:T(8,128)(2,1)S(1)} %pad_maximum_fusion) | data formatting | bytes 2359296 | tf_op jit(solution)/shard_map/stack | solution.py:31
  112.4 10.7 %reshape.1359 = bf16[4,2,73728]{2,1,0:T(2,128)(2,1)} reshape(bf16[3072,2,4,24]{3,2,1,0:T(4,128)(2,1)} %bitcast.532) | data formatting | bytes 2359296
  128.0 14.4 %all-to-all-done.1 = bf16[4,2,73728]{2,1,0:T(2,128)(2,1)S(1)} async-done(((bf16[4,2,73728]{2,1,0:T(2,128)(2,1)}), bf16[4,2,73728]{2,1,0:T(2,128)(2,1)S(1)}, u32[]{:S(2)}, u32[]{:S(2)}) %all-to-all-start.1) | async-done | bytes 1179680 | tf_op jit(solution)/shard_map/all_to_all | solution.py:120
  230.2 10.3 %reshape.1361 = bf16[4,2,73728]{2,1,0:T(2,128)(2,1)} reshape(bf16[3072,2,4,24]{3,2,1,0:T(4,128)(2,1)} %bitcast.533) | data formatting | bytes 2359296
  263.9 10.5 %copy.562 = bf16[24,3,8192]{0,1,2:T(4,128)(2,1)} copy(bf16[24,3,8192]{0,2,1:T(8,128)(2,1)} %bitcast.534) | data formatting | bytes 2359296 | tf_op jit(solution)/shard_map/convert_element_type | solution.py:100
  274.4 10.9 %reshape.1367 = bf16[8,2,36864]{2,1,0:T(2,128)(2,1)} reshape(bf16[8192,3,24]{2,1,0:T(4,128)(2,1)} %bitcast.521) | data formatting | bytes 2359296
  289.8 10.2 %reshape.1362 = bf16[3072,2,4,24]{3,2,1,0:T(4,128)(2,1)} reshape(bf16[4,2,73728]{2,1,0:T(2,128)(2,1)S(1)} %all-to-all-done.2) | data formatting | bytes 2359296
  315.5 12.2 %copy.563 = bf16[24,4,8192]{0,1,2:T(4,128)(2,1)} copy(bf16[24,4,8192]{0,2,1:T(8,128)(2,1)} %bitcast.526) | data formatting | bytes 3145728 | tf_op jit(solution)/shard_map/convert_element_type | solution.py:100
  327.7 12.6 %reshape.1363 = bf16[8,2,49152]{2,1,0:T(2,128)(2,1)} reshape(bf16[8192,4,24]{2,1,0:T(4,128)(2,1)} %bitcast.527) | data formatting | bytes 3145728
  346.6 11.4 %reshape.1368 = bf16[8192,3,24]{2,1,0:T(4,128)(2,1)} reshape(bf16[8,2,36864]{2,1,0:T(2,128)(2,1)} %all-to-all-done.7) | data formatting | bytes 2359296
  358.0 11.2 %copy.559 = bf16[24,3,8,1024]{0,2,3,1:T(8,128)(2,1)} copy(bf16[24,3,8,1024]{0,1,3,2:T(4,128)(2,1)} %bitcast.522) | data formatting | bytes 2359296 | tf_op jit(solution)/shard_map/all_to_all | solution.py:134
  383.9 13.1 %reshape.1364 = bf16[8192,4,24]{2,1,0:T(4,128)(2,1)} reshape(bf16[8,2,49152]{2,1,0:T(2,128)(2,1)S(1)} %all-to-all-done.3) | data formatting | bytes 3145728
  397.0 12.1 %copy.558 = bf16[24,4,8,1024]{0,2,3,1:T(8,128)(2,1)} copy(bf16[24,4,8,1024]{0,1,3,2:T(4,128)(2,1)} %bitcast.528) | data formatting | bytes 3145728 | tf_op jit(solution)/shard_map/all_to_all | solution.py:134
  435.6 17.4 %all-to-all-done.4 = bf16[192,2,1024]{2,1,0:T(2,128)(2,1)S(1)} async-done(((bf16[192,2,1024]{2,1,0:T(2,128)(2,1)}), bf16[192,2,1024]{2,1,0:T(2,128)(2,1)S(1)}, u32[]{:S(2)}, u32[]{:S(2)}) %all-to-all-start.4) | async-done | bytes 786464 | tf_op jit(solution)/shard_map/all_to_all | solution.py:119
  464.9 19.1 %copy.566 = bf16[24,2,2,3072]{0,1,2,3:T(2,128)(2,1)S(1)} copy(bf16[24,2,2,3072]{0,3,1,2:T(8,128)(2,1)S(1)} %pad_maximum_fusion.3) | data formatting | bytes 1179648 | tf_op jit(solution)/shard_map/stack | solution.py:31
  526.8 16.3 %all-to-all-done.8 = bf16[192,3,1024]{2,1,0:T(4,128)(2,1)} async-done(((bf16[192,3,1024]{2,1,0:T(4,128)(2,1)}), bf16[192,3,1024]{2,1,0:T(4,128)(2,1)}, u32[]{:S(2)}, u32[]{:S(2)}) %all-to-all-start.8) | async-done | bytes 1179680 | tf_op jit(solution)/shard_map/all_to_all | solution.py:119
  568.7 42.6 %copy.565 = bf16[24,3,2,3072]{0,2,1,3:T(2,128)(2,1)} copy(bf16[24,3,2,3072]{0,3,1,2:T(8,128)(2,1)S(1)} %pad_maximum_fusion.1) | data formatting | bytes 1769472 | tf_op jit(solution)/shard_map/stack | solution.py:31
  696.2 18.3 %all_to_all.120 = bf16[4,2,73728]{2,1,0:T(2,128)(2,1)S(1)} all-to-all(bf16[4,2,73728]{2,1,0:T(2,128)(2,1)S(1)} %reshape.1373), channel_id=1, replica_groups=mesh['row'=4,'col'=8] {'row'}, dimensions={0} | all-to-all | bytes 2359296 | tf_op jit(solution)/shard_map/all_to_all | solution.py:133
  740.3 12.2 %copy.561 = bf16[24,4,8192]{0,1,2:T(4,128)(2,1)} copy(bf16[24,4,8192]{0,2,1:T(8,128)(2,1)} %bitcast.529) | data formatting | bytes 3145728 | tf_op jit(solution)/shard_map/convert_element_type | solution.py:100
  752.4 11.9 %reshape.1375 = bf16[8,2,49152]{2,1,0:T(2,128)(2,1)S(1)} reshape(bf16[8192,4,24]{2,1,0:T(4,128)(2,1)} %bitcast.530) | data formatting | bytes 3145728
  764.4 40.3 %all_to_all.121 = bf16[8,2,49152]{2,1,0:T(2,128)(2,1)S(1)} all-to-all(bf16[8,2,49152]{2,1,0:T(2,128)(2,1)S(1)} %reshape.1375), channel_id=1, replica_groups=mesh['row'=4,'col'=8] {'col'}, dimensions={0} | all-to-all | bytes 3145728 | tf_op jit(solution)/shard_map/all_to_all | solution.py:134
  804.7 12.9 %reshape.1376 = bf16[8192,4,24]{2,1,0:T(4,128)(2,1)} reshape(bf16[8,2,49152]{2,1,0:T(2,128)(2,1)S(1)} %all_to_all.121) | data formatting | bytes 3145728
  817.6 12.1 %copy.557 = bf16[24,4,8,1024]{0,2,3,1:T(8,128)(2,1)} copy(bf16[24,4,8,1024]{0,1,3,2:T(4,128)(2,1)} %bitcast.531) | data formatting | bytes 3145728 | tf_op jit(solution)/shard_map/all_to_all | solution.py:134
  (296 shorter events, 447.6 us)
Async XLA Ops:
  13.6 44.5 %all-to-all-start = ((bf16[192,4,1024]{2,1,0:T(4,128)(2,1)}), bf16[192,4,1024]{2,1,0:T(4,128)(2,1)S(1)}, u32[]{:S(2)}, u32[]{:S(2)}) async-start(bf16[192,4,1024]{2,1,0:T(4,128)(2,1)} %copy.375), calls=%async_computation | async-start | bytes 3145728 | tf_op jit(solution)/shard_map/all_to_all | solution.py:119
  21.3 198.4 %copy-start.27 = (bf16[1,4,8,24]{3,2,1,0:T(8,128)(2,1)}, bf16[1,4,8,24]{3,2,1,0:T(8,128)(2,1)S(1)}, u32[]{:S(2)}) copy-start(bf16[1,4,8,24]{3,2,1,0:T(8,128)(2,1)S(1)} %get-tuple-element.50) | copy-start | bytes 4612
  21.3 198.4 %copy-start.31 = (bf16[1,4,8,24]{3,2,1,0:T(8,128)(2,1)}, bf16[1,4,8,24]{3,2,1,0:T(8,128)(2,1)S(1)}, u32[]{:S(2)}) copy-start(bf16[1,4,8,24]{3,2,1,0:T(8,128)(2,1)S(1)} %get-tuple-element.51) | copy-start | bytes 4612
  123.1 19.3 %all-to-all-start.1 = ((bf16[4,2,73728]{2,1,0:T(2,128)(2,1)}), bf16[4,2,73728]{2,1,0:T(2,128)(2,1)S(1)}, u32[]{:S(2)}, u32[]{:S(2)}) async-start(bf16[4,2,73728]{2,1,0:T(2,128)(2,1)} %reshape.1359), calls=%async_computation.1 | async-start | bytes 2359296 | tf_op jit(solution)/shard_map/all_to_all | solution.py:120
  126.6 51.7 %copy-start.38 = (f32[24]{0:T(128)}, f32[24]{0:T(128)S(1)}, u32[]{:S(2)}) copy-start(f32[24]{0:T(128)S(1)} %add_convert_fusion.2) | copy-start | bytes 292
  126.9 51.4 %copy-start.18 = (f32[2304]{0:T(1024)}, f32[2304]{0:T(1024)S(1)}, u32[]{:S(2)}) copy-start(f32[2304]{0:T(1024)S(1)} %reshape.1314) | copy-start | bytes 27652
  215.9 24.5 %all-to-all-start.6 = ((bf16[4,2,55296]{2,1,0:T(2,128)(2,1)}), bf16[4,2,55296]{2,1,0:T(2,128)(2,1)S(1)}, u32[]{:S(2)}, u32[]{:S(2)}) async-start(bf16[4,2,55296]{2,1,0:T(2,128)(2,1)} %reshape.1365), calls=%async_computation.6 | async-start | bytes 1769472 | tf_op jit(solution)/shard_map/all_to_all | solution.py:133
  240.5 44.9 %all-to-all-start.2 = ((bf16[4,2,73728]{2,1,0:T(2,128)(2,1)}), bf16[4,2,73728]{2,1,0:T(2,128)(2,1)S(1)}, u32[]{:S(2)}, u32[]{:S(2)}) async-start(bf16[4,2,73728]{2,1,0:T(2,128)(2,1)} %reshape.1361), calls=%async_computation.2 | async-start | bytes 2359296 | tf_op jit(solution)/shard_map/all_to_all | solution.py:133
  285.3 55.0 %all-to-all-start.7 = ((bf16[8,2,36864]{2,1,0:T(2,128)(2,1)}), bf16[8,2,36864]{2,1,0:T(2,128)(2,1)}, u32[]{:S(2)}, u32[]{:S(2)}) async-start(bf16[8,2,36864]{2,1,0:T(2,128)(2,1)} %reshape.1367), calls=%async_computation.7 | async-start | bytes 2359296 | tf_op jit(solution)/shard_map/all_to_all | solution.py:134
  289.8 10.2 %copy-start.22 = (bf16[1,8,64,4,96]{4,2,3,1,0:T(8,128)(2,1)S(1)}, bf16[1,8,64,4,96]{4,2,3,1,0:T(8,128)(2,1)}, u32[]{:S(2)}) copy-start(bf16[1,8,64,4,96]{4,2,3,1,0:T(8,128)(2,1)} %get-tuple-element.46) | copy-start | bytes 1179652
  289.8 10.2 %copy-start.25 = (bf16[1,8,64,4,96]{4,2,3,1,0:T(8,128)(2,1)S(1)}, bf16[1,8,64,4,96]{4,2,3,1,0:T(8,128)(2,1)}, u32[]{:S(2)}) copy-start(bf16[1,8,64,4,96]{4,2,3,1,0:T(8,128)(2,1)} %get-tuple-element.47) | copy-start | bytes 1179652
  340.4 43.5 %all-to-all-start.3 = ((bf16[8,2,49152]{2,1,0:T(2,128)(2,1)}), bf16[8,2,49152]{2,1,0:T(2,128)(2,1)S(1)}, u32[]{:S(2)}, u32[]{:S(2)}) async-start(bf16[8,2,49152]{2,1,0:T(2,128)(2,1)} %reshape.1363), calls=%async_computation.3 | async-start | bytes 3145728 | tf_op jit(solution)/shard_map/all_to_all | solution.py:134
  428.9 24.2 %all-to-all-start.4 = ((bf16[192,2,1024]{2,1,0:T(2,128)(2,1)}), bf16[192,2,1024]{2,1,0:T(2,128)(2,1)S(1)}, u32[]{:S(2)}, u32[]{:S(2)}) async-start(bf16[192,2,1024]{2,1,0:T(2,128)(2,1)} %copy.405), calls=%async_computation.4 | async-start | bytes 1572864 | tf_op jit(solution)/shard_map/all_to_all | solution.py:119
  488.7 13.0 %all-to-all-start.5 = ((bf16[4,2,36864]{2,1,0:T(2,128)(2,1)}), bf16[4,2,36864]{2,1,0:T(2,128)(2,1)S(1)}, u32[]{:S(2)}, u32[]{:S(2)}) async-start(bf16[4,2,36864]{2,1,0:T(2,128)(2,1)} %reshape.1371), calls=%async_computation.5 | async-start | bytes 1179648 | tf_op jit(solution)/shard_map/all_to_all | solution.py:120
  501.6 41.5 %all-to-all-start.8 = ((bf16[192,3,1024]{2,1,0:T(4,128)(2,1)}), bf16[192,3,1024]{2,1,0:T(4,128)(2,1)}, u32[]{:S(2)}, u32[]{:S(2)}) async-start(bf16[192,3,1024]{2,1,0:T(4,128)(2,1)} %copy.437), calls=%async_computation.8 | async-start | bytes 3145728 | tf_op jit(solution)/shard_map/all_to_all | solution.py:119
  611.3 12.9 %copy-start.2 = (f32[24,4,2,2304]{3,0,1,2:T(8,128)S(1)}, f32[24,4,2,2304]{3,0,1,2:T(8,128)}, u32[]{:S(2)}) copy-start(f32[24,4,2,2304]{3,0,1,2:T(8,128)} %copy-done.1) | copy-start | bytes 5308420
  611.3 12.9 %copy-start.14 = (f32[24,2304]{1,0:T(8,128)S(1)}, f32[24,2304]{1,0:T(8,128)}, u32[]{:S(2)}) copy-start(f32[24,2304]{1,0:T(8,128)} %get-tuple-element.40) | copy-start | bytes 663556
  611.3 12.9 %copy-start.15 = (f32[24,2304]{1,0:T(8,128)S(1)}, f32[24,2304]{1,0:T(8,128)}, u32[]{:S(2)}) copy-start(f32[24,2304]{1,0:T(8,128)} %get-tuple-element.42) | copy-start | bytes 663556
  611.3 12.9 %copy-start.16 = (f32[24,2304]{1,0:T(8,128)S(1)}, f32[24,2304]{1,0:T(8,128)}, u32[]{:S(2)}) copy-start(f32[24,2304]{1,0:T(8,128)} %get-tuple-element.45) | copy-start | bytes 663556
  611.3 12.9 %copy-start.37 = (pred[24,2304]{1,0:T(8,128)(4,1)S(1)}, pred[24,2304]{1,0:T(8,128)(4,1)}, u32[]{:S(2)}) copy-start(pred[24,2304]{1,0:T(8,128)(4,1)} %and_and_fusion) | copy-start | bytes 165892
  619.5 17.4 %all-to-all-start.9 = ((bf16[4,2,55296]{2,1,0:T(2,128)(2,1)}), bf16[4,2,55296]{2,1,0:T(2,128)(2,1)}, u32[]{:S(2)}, u32[]{:S(2)}) async-start(bf16[4,2,55296]{2,1,0:T(2,128)(2,1)} %reshape.1369), calls=%async_computation.9 | async-start | bytes 1769472 | tf_op jit(solution)/shard_map/all_to_all | solution.py:120
  645.6 9.0 %copy-start.33 = (bf16[1,4,8,24]{3,2,1,0:T(8,128)(2,1)S(1)}, bf16[1,4,8,24]{3,2,1,0:T(8,128)(2,1)}, u32[]{:S(2)}) copy-start(bf16[1,4,8,24]{3,2,1,0:T(8,128)(2,1)} %copy-done.31) | copy-start | bytes 4612
  714.5 10.2 %copy-start.23 = (bf16[1,8,64,4,96]{4,2,3,1,0:T(8,128)(2,1)S(1)}, bf16[1,8,64,4,96]{4,2,3,1,0:T(8,128)(2,1)}, u32[]{:S(2)}) copy-start(bf16[1,8,64,4,96]{4,2,3,1,0:T(8,128)(2,1)} %get-tuple-element.46) | copy-start | bytes 1179652
  714.5 10.2 %copy-start.26 = (bf16[1,8,64,4,96]{4,2,3,1,0:T(8,128)(2,1)S(1)}, bf16[1,8,64,4,96]{4,2,3,1,0:T(8,128)(2,1)}, u32[]{:S(2)}) copy-start(bf16[1,8,64,4,96]{4,2,3,1,0:T(8,128)(2,1)} %get-tuple-element.47) | copy-start | bytes 1179652
  (26 other events, 91.4 us)
where the time goes:
time: 853 us; the launch traced here: 845 us
  local copies, waits for them, and re-layouts  566 us (66%)
  waiting for transfers between devices  89.2 us (10%)
  blocking collectives  58.6 us (7%)
  starting transfers between devices  46 us (5%)
  matrix products  41.3 us (5%)
  other arithmetic  40.8 us (5%)
    unnamed x100, local copies, waits for them, and re-layouts  187 us
    another operation x9, local copies, waits for them, and re-layouts, pair_sum(): return jnp.stack([real_part, imag_part], axis=stack_axis)  126 us
    all_to_all x3, waiting for transfers between devices, forward(): lax.all_to_all(x_lines, 'col', split_axis=0, concat_axis=2, tiled=True)  60.6 us
    all_to_all x1, blocking collectives, inverse(): lax.all_to_all(spread, 'col', split_axis=2, concat_axis=0, tiled=True)  40.3 us
    all_to_all x3, local copies, waits for them, and re-layouts, inverse(): lax.all_to_all(spread, 'col', split_axis=2, concat_axis=0, tiled=True)  35.3 us
    convert_element_type x3, local copies, waits for them, and re-layouts, back_y(): joined = pair_sum(pieces, 1, 3).astype(jnp.bfloat16)  34.9 us
    reshape x3, local copies, waits for them, and re-layouts, back_x(): shaped = incoming.reshape(KC, field_count, 2, rows_y, planes)  27.1 us
    all_to_all x3, waiting for transfers between devices, forward(): lax.all_to_all(spread, 'row', split_axis=3, concat_axis=3, tiled=True)  25.1 us
  transfers between devices with their start and end apart: 10, of which 7 were waited for; matrix products, arithmetic and copies ran while one was open for 23% of the time, Pallas kernels for 0%

commit v1 on v0

--- a/solution.py
+++ b/solution.py
@@ -131,7 +131,14 @@
             .reshape(kx_local, field_count, 2, total_z * ky_local)
         )
         spread = back_y(lax.all_to_all(z_planes, "row", split_axis=3, concat_axis=3, tiled=True))
-        return back_x(lax.all_to_all(spread, "col", split_axis=2, concat_axis=0, tiled=True))
+        return back_x(
+            jnp.concatenate(
+                lax.all_to_all(
+                    jnp.stack(jnp.split(spread, lax.axis_size("col"), axis=2)), "col", 0, 0
+                ),
+                axis=0,
+            )
+        )
 
     spectra = forward(jnp.concatenate([phase[None], velocity], axis=0))
     wave_x = (lax.axis_index("col") * kx_local + jnp.arange(kx_local, dtype=jnp.int32)).astype(

time: 853 us -> 815 us (0.955)
  local copies, waits for them, and re-layouts: 566 us -> 514 us
  waiting for transfers between devices: 89.2 us -> 104 us
    another operation x12 -> x45, local copies, waits for them, and re-layouts: 16.3 us -> 94.6 us  [the longest x30 51.7 us: inverse(): jnp.stack(jnp.split(spread, lax.axis_size('col'), axis=2))]
    unnamed x100 -> x139, local copies, waits for them, and re-layouts: 187 us -> 130 us
    convert_element_type x3 -> x0, local copies, waits for them, and re-layouts: 34.9 us -> none  [back_y(): joined = pair_sum(pieces, 1, 3).astype(jnp.bfloat16)]
    reshape x3 -> x0, local copies, waits for them, and re-layouts: 27.1 us -> none  [back_x(): shaped = incoming.reshape(KC, field_count, 2, rows_y, planes)]
    all_to_all x2, waiting for transfers between devices: 3.51 us -> 18.7 us  [inverse(): lax.all_to_all(jnp.stack(jnp.split(spread, lax.axis_size('col'), axis=2))...]
    all_to_all x3, local copies, waits for them, and re-layouts: 35.3 us -> 22.6 us  [inverse(): lax.all_to_all(jnp.stack(jnp.split(spread, lax.axis_size('col'), axis=2))...]
  transfers between devices with their start and end apart: 10 -> 10, of which waited for: 7 -> 7; matrix products, arithmetic and copies ran while one was open for 23% -> 22% of each run, Pallas kernels for 0% -> 0%
where the time goes in v1:
time: 815 us; the launch traced here: 807 us
  local copies, waits for them, and re-layouts  514 us (63%)
  waiting for transfers between devices  104 us (13%)
  blocking collectives  59 us (7%)
  starting transfers between devices  45.8 us (6%)
  matrix products  41.4 us (5%)
  other arithmetic  39.7 us (5%)
    unnamed x139, local copies, waits for them, and re-layouts  130 us
    another operation x9, local copies, waits for them, and re-layouts, pair_sum(): return jnp.stack([real_part, imag_part], axis=stack_axis)  126 us
    all_to_all x3, waiting for transfers between devices, forward(): lax.all_to_all(x_lines, 'col', split_axis=0, concat_axis=2, tiled=True)  60.6 us
    another operation x30, local copies, waits for them, and re-layouts, inverse(): jnp.stack(jnp.split(spread, lax.axis_size('col'), axis=2))  51.7 us
    all_to_all x1, blocking collectives, inverse(): lax.all_to_all(jnp.stack(jnp.split(spread, lax.axis_size('col'), axis=2))...  40.7 us
    another operation x3, local copies, waits for them, and re-layouts, back_x(): shaped = incoming.reshape(KC, field_count, 2, rows_y, planes)  26.6 us
    all_to_all x3, waiting for transfers between devices, forward(): lax.all_to_all(spread, 'row', split_axis=3, concat_axis=3, tiled=True)  25.1 us
    reshape x3, local copies, waits for them, and re-layouts, along_z(): incoming.reshape(incoming.shape[0], field_count, 2, row_count, ky_local,...  24.7 us
  transfers between devices with their start and end apart: 10, of which 7 were waited for; matrix products, arithmetic and copies ran while one was open for 22% of the time, Pallas kernels for 0%

profile of v1, /device:TPU:0, one launch (start us, length us, event | category | flops | bytes accessed | tf_op | source)
XLA Modules:
  0.0 806.6 jit_solution(3480015780920626249)
XLA Ops:
  30.0 26.8 %all-to-all-done = bf16[192,4,1024]{2,1,0:T(4,128)(2,1)S(1)} async-done(((bf16[192,4,1024]{2,1,0:T(4,128)(2,1)}), bf16[192,4,1024]{2,1,0:T(4,128)(2,1)S(1)}, u32[]{:S(2)}, u32[]{:S(2)}) %all-to-all-start) | async-done | bytes 1572896 | tf_op jit(solution)/shard_map/all_to_all | solution.py:119
  63.1 8.6 %copy.416 = bf16[24,4,8,2,64,8]{4,0,2,5,3,1:T(8,128)(2,1)S(1)} copy(bf16[24,4,8,2,64,8]{0,5,4,3,2,1:T(8,128)(2,1)} %bitcast.546) | data formatting | bytes 3145728 | tf_op jit(solution)/shard_map/reshape | solution.py:78
  85.9 25.2 %copy.608 = bf16[24,4,2,3072]{0,1,2,3:T(4,128)(2,1)} copy(bf16[24,4,2,3072]{0,3,1,2:T(8,128)(2,1)S(1)} %pad_maximum_fusion) | data formatting | bytes 2359296 | tf_op jit(solution)/shard_map/stack | solution.py:31
  111.1 10.5 %reshape.1344 = bf16[4,2,73728]{2,1,0:T(2,128)(2,1)} reshape(bf16[3072,2,4,24]{3,2,1,0:T(4,128)(2,1)} %bitcast.548) | data formatting | bytes 2359296
  126.5 14.3 %all-to-all-done.1 = bf16[4,2,73728]{2,1,0:T(2,128)(2,1)S(1)} async-done(((bf16[4,2,73728]{2,1,0:T(2,128)(2,1)}), bf16[4,2,73728]{2,1,0:T(2,128)(2,1)S(1)}, u32[]{:S(2)}, u32[]{:S(2)}) %all-to-all-start.1) | async-done | bytes 1179680 | tf_op jit(solution)/shard_map/all_to_all | solution.py:120
  140.9 10.2 %reshape.1345 = bf16[3072,2,4,24]{3,2,1,0:T(4,128)(2,1)} reshape(bf16[4,2,73728]{2,1,0:T(2,128)(2,1)S(1)} %all-to-all-done.1) | data formatting | bytes 2359296
  151.0 9.8 %copy.421 = bf16[24,4,2,4,96,8]{4,5,3,2,1,0:T(8,128)(2,1)S(1)} copy(bf16[24,4,2,4,96,8]{0,1,2,5,4,3:T(4,128)(2,1)} %bitcast.552) | data formatting | bytes 2359296 | tf_op jit(solution)/shard_map/reshape | solution.py:87
  205.4 8.0 reshape.1348
  227.6 10.3 %reshape.1346 = bf16[4,2,73728]{2,1,0:T(2,128)(2,1)} reshape(bf16[3072,2,4,24]{3,2,1,0:T(4,128)(2,1)} %bitcast.549) | data formatting | bytes 2359296
  290.3 10.2 %reshape.1347 = bf16[3072,2,4,24]{3,2,1,0:T(4,128)(2,1)} reshape(bf16[4,2,73728]{2,1,0:T(2,128)(2,1)S(1)} %all-to-all-done.2) | data formatting | bytes 2359296
  363.7 18.7 %all-to-all-done.3 = bf16[8,24,4,1024]{3,1,2,0:T(8,128)(2,1)S(1)} async-done(((bf16[8,24,4,1024]{3,1,2,0:T(8,128)(2,1)}), bf16[8,24,4,1024]{3,1,2,0:T(8,128)(2,1)S(1)}, u32[]{:S(2)}, u32[]{:S(2)}) %all-to-all-start.3) | async-done | bytes 1572896 | tf_op jit(solution)/shard_map/all_to_all | solution.py:136
  390.0 9.6 %reshape_reshape.9 = bf16[192,4,2,64,8]{0,4,3,2,1:T(8,128)(2,1)S(1)} reshape(bf16[8,24,4,1024]{1,0,3,2:T(8,128)(2,1)} %copy.445) | data formatting | bytes 3145728 | tf_op jit(solution)/shard_map/reshape;reshape | solution.py:105
  416.1 17.4 %all-to-all-done.4 = bf16[192,2,1024]{2,1,0:T(2,128)(2,1)S(1)} async-done(((bf16[192,2,1024]{2,1,0:T(2,128)(2,1)}), bf16[192,2,1024]{2,1,0:T(2,128)(2,1)S(1)}, u32[]{:S(2)}, u32[]{:S(2)}) %all-to-all-start.4) | async-done | bytes 786464 | tf_op jit(solution)/shard_map/all_to_all | solution.py:119
  445.3 19.1 %copy.610 = bf16[24,2,2,3072]{0,1,2,3:T(2,128)(2,1)S(1)} copy(bf16[24,2,2,3072]{0,3,1,2:T(8,128)(2,1)S(1)} %pad_maximum_fusion.3) | data formatting | bytes 1179648 | tf_op jit(solution)/shard_map/stack | solution.py:31
  507.3 16.3 %all-to-all-done.8 = bf16[192,3,1024]{2,1,0:T(4,128)(2,1)} async-done(((bf16[192,3,1024]{2,1,0:T(4,128)(2,1)}), bf16[192,3,1024]{2,1,0:T(4,128)(2,1)}, u32[]{:S(2)}, u32[]{:S(2)}) %all-to-all-start.8) | async-done | bytes 1179680 | tf_op jit(solution)/shard_map/all_to_all | solution.py:119
  549.2 42.8 %copy.609 = bf16[24,3,2,3072]{0,2,1,3:T(2,128)(2,1)} copy(bf16[24,3,2,3072]{0,3,1,2:T(8,128)(2,1)S(1)} %pad_maximum_fusion.1) | data formatting | bytes 1769472 | tf_op jit(solution)/shard_map/stack | solution.py:31
  591.9 8.1 reshape.1350
  617.3 8.7 %reshape.1351 = bf16[3072,3,2,24]{3,2,1,0:T(2,128)(2,1)} reshape(bf16[4,2,55296]{2,1,0:T(2,128)(2,1)} %all-to-all-done.9) | data formatting | bytes 1769472
  625.9 9.0 %copy.496 = bf16[24,3,2,4,96,8]{4,5,3,2,1,0:T(8,128)(2,1)S(1)} copy(bf16[24,3,2,4,96,8]{0,2,1,5,4,3:T(2,128)(2,1)} %bitcast.554) | data formatting | bytes 1769472 | tf_op jit(solution)/shard_map/reshape | solution.py:87
  666.9 9.8 %reshape.1354 = bf16[4,2,73728]{2,1,0:T(2,128)(2,1)S(1)} reshape(bf16[3072,2,4,24]{3,2,1,0:T(4,128)(2,1)} %bitcast.551) | data formatting | bytes 2359296
  676.7 18.3 %all_to_all.90 = bf16[4,2,73728]{2,1,0:T(2,128)(2,1)S(1)} all-to-all(bf16[4,2,73728]{2,1,0:T(2,128)(2,1)S(1)} %reshape.1354), channel_id=1, replica_groups=mesh['row'=4,'col'=8] {'row'}, dimensions={0} | all-to-all | bytes 2359296 | tf_op jit(solution)/shard_map/all_to_all | solution.py:133
  694.9 10.2 %reshape.1355 = bf16[3072,2,4,24]{3,2,1,0:T(4,128)(2,1)} reshape(bf16[4,2,73728]{2,1,0:T(2,128)(2,1)S(1)} %all_to_all.90) | data formatting | bytes 2359296
  742.7 40.7 %all_to_all.91 = bf16[8,24,4,1024]{3,1,2,0:T(8,128)(2,1)S(1)} all-to-all(bf16[8,24,4,1024]{3,1,2,0:T(8,128)(2,1)} %constant_dynamic-update-slice_fusion.16), channel_id=1, replica_groups=mesh['row'=4,'col'=8] {'col'}, dimensions={0} | all-to-all | bytes 3145728 | tf_op jit(solution)/shard_map/all_to_all | solution.py:136
  791.0 9.6 %reshape_reshape.11 = bf16[192,4,2,64,8]{0,4,3,2,1:T(8,128)(2,1)S(1)} reshape(bf16[8,24,4,1024]{1,0,3,2:T(8,128)(2,1)} %copy.520) | data formatting | bytes 3145728 | tf_op jit(solution)/shard_map/reshape;reshape | solution.py:105
  (362 shorter events, 431.8 us)
Async XLA Ops:
  12.4 44.4 %all-to-all-start = ((bf16[192,4,1024]{2,1,0:T(4,128)(2,1)}), bf16[192,4,1024]{2,1,0:T(4,128)(2,1)S(1)}, u32[]{:S(2)}, u32[]{:S(2)}) async-start(bf16[192,4,1024]{2,1,0:T(4,128)(2,1)} %copy.413), calls=%async_computation | async-start | bytes 3145728 | tf_op jit(solution)/shard_map/all_to_all | solution.py:119
  19.9 157.0 %copy-start.50 = (f32[24]{0:T(128)}, f32[24]{0:T(128)S(1)}, u32[]{:S(2)}) copy-start(f32[24]{0:T(128)S(1)} %add_convert_fusion.2) | copy-start | bytes 292
  20.1 197.0 %copy-start.39 = (bf16[1,4,8,24]{3,2,1,0:T(8,128)(2,1)}, bf16[1,4,8,24]{3,2,1,0:T(8,128)(2,1)S(1)}, u32[]{:S(2)}) copy-start(bf16[1,4,8,24]{3,2,1,0:T(8,128)(2,1)S(1)} %get-tuple-element.74) | copy-start | bytes 4612
  20.1 197.0 %copy-start.43 = (bf16[1,4,8,24]{3,2,1,0:T(8,128)(2,1)}, bf16[1,4,8,24]{3,2,1,0:T(8,128)(2,1)S(1)}, u32[]{:S(2)}) copy-start(bf16[1,4,8,24]{3,2,1,0:T(8,128)(2,1)S(1)} %get-tuple-element.75) | copy-start | bytes 4612
  121.5 19.3 %all-to-all-start.1 = ((bf16[4,2,73728]{2,1,0:T(2,128)(2,1)}), bf16[4,2,73728]{2,1,0:T(2,128)(2,1)S(1)}, u32[]{:S(2)}, u32[]{:S(2)}) async-start(bf16[4,2,73728]{2,1,0:T(2,128)(2,1)} %reshape.1344), calls=%async_computation.1 | async-start | bytes 2359296 | tf_op jit(solution)/shard_map/all_to_all | solution.py:120
  125.4 51.6 %copy-start.26 = (f32[2304]{0:T(1024)}, f32[2304]{0:T(1024)S(1)}, u32[]{:S(2)}) copy-start(f32[2304]{0:T(1024)S(1)} %reshape.1302) | copy-start | bytes 27652
  213.4 24.5 %all-to-all-start.6 = ((bf16[4,2,55296]{2,1,0:T(2,128)(2,1)}), bf16[4,2,55296]{2,1,0:T(2,128)(2,1)S(1)}, u32[]{:S(2)}, u32[]{:S(2)}) async-start(bf16[4,2,55296]{2,1,0:T(2,128)(2,1)} %reshape.1348), calls=%async_computation.6 | async-start | bytes 1769472 | tf_op jit(solution)/shard_map/all_to_all | solution.py:133
  237.9 47.7 %all-to-all-start.2 = ((bf16[4,2,73728]{2,1,0:T(2,128)(2,1)}), bf16[4,2,73728]{2,1,0:T(2,128)(2,1)S(1)}, u32[]{:S(2)}, u32[]{:S(2)}) async-start(bf16[4,2,73728]{2,1,0:T(2,128)(2,1)} %reshape.1346), calls=%async_computation.2 | async-start | bytes 2359296 | tf_op jit(solution)/shard_map/all_to_all | solution.py:133
  285.5 53.3 %all-to-all-start.7 = ((bf16[8,24,3,1024]{3,1,2,0:T(8,128)(2,1)}), bf16[8,24,3,1024]{3,1,2,0:T(8,128)(2,1)}, u32[]{:S(2)}, u32[]{:S(2)}) async-start(bf16[8,24,3,1024]{3,1,2,0:T(8,128)(2,1)} %constant_dynamic-update-slice_fusion.8), calls=%async_computation.7 | async-start | bytes 2359296 | tf_op jit(solution)/shard_map/all_to_all | solution.py:136
  290.3 10.2 %copy-start.33 = (bf16[1,8,64,4,96]{4,2,3,1,0:T(8,128)(2,1)S(1)}, bf16[1,8,64,4,96]{4,2,3,1,0:T(8,128)(2,1)}, u32[]{:S(2)}) copy-start(bf16[1,8,64,4,96]{4,2,3,1,0:T(8,128)(2,1)} %get-tuple-element.70) | copy-start | bytes 1179652
  290.3 10.2 %copy-start.36 = (bf16[1,8,64,4,96]{4,2,3,1,0:T(8,128)(2,1)S(1)}, bf16[1,8,64,4,96]{4,2,3,1,0:T(8,128)(2,1)}, u32[]{:S(2)}) copy-start(bf16[1,8,64,4,96]{4,2,3,1,0:T(8,128)(2,1)} %get-tuple-element.71) | copy-start | bytes 1179652
  338.9 43.5 %all-to-all-start.3 = ((bf16[8,24,4,1024]{3,1,2,0:T(8,128)(2,1)}), bf16[8,24,4,1024]{3,1,2,0:T(8,128)(2,1)S(1)}, u32[]{:S(2)}, u32[]{:S(2)}) async-start(bf16[8,24,4,1024]{3,1,2,0:T(8,128)(2,1)} %constant_dynamic-update-slice_fusion), calls=%async_computation.3 | async-start | bytes 3145728 | tf_op jit(solution)/shard_map/all_to_all | solution.py:136
  409.3 24.2 %all-to-all-start.4 = ((bf16[192,2,1024]{2,1,0:T(2,128)(2,1)}), bf16[192,2,1024]{2,1,0:T(2,128)(2,1)S(1)}, u32[]{:S(2)}, u32[]{:S(2)}) async-start(bf16[192,2,1024]{2,1,0:T(2,128)(2,1)} %copy.450), calls=%async_computation.4 | async-start | bytes 1572864 | tf_op jit(solution)/shard_map/all_to_all | solution.py:119
  469.1 13.0 %all-to-all-start.5 = ((bf16[4,2,36864]{2,1,0:T(2,128)(2,1)}), bf16[4,2,36864]{2,1,0:T(2,128)(2,1)S(1)}, u32[]{:S(2)}, u32[]{:S(2)}) async-start(bf16[4,2,36864]{2,1,0:T(2,128)(2,1)} %reshape.1352), calls=%async_computation.5 | async-start | bytes 1179648 | tf_op jit(solution)/shard_map/all_to_all | solution.py:120
  482.1 41.5 %all-to-all-start.8 = ((bf16[192,3,1024]{2,1,0:T(4,128)(2,1)}), bf16[192,3,1024]{2,1,0:T(4,128)(2,1)}, u32[]{:S(2)}, u32[]{:S(2)}) async-start(bf16[192,3,1024]{2,1,0:T(4,128)(2,1)} %copy.488), calls=%async_computation.8 | async-start | bytes 3145728 | tf_op jit(solution)/shard_map/all_to_all | solution.py:119
  591.9 12.6 %copy-start.15 = (f32[24,2304]{1,0:T(8,128)S(1)}, f32[24,2304]{1,0:T(8,128)}, u32[]{:S(2)}) copy-start(f32[24,2304]{1,0:T(8,128)} %get-tuple-element.64) | copy-start | bytes 663556
  591.9 12.6 %copy-start.16 = (f32[24,2304]{1,0:T(8,128)S(1)}, f32[24,2304]{1,0:T(8,128)}, u32[]{:S(2)}) copy-start(f32[24,2304]{1,0:T(8,128)} %get-tuple-element.66) | copy-start | bytes 663556
  591.9 12.6 %copy-start.17 = (f32[24,2304]{1,0:T(8,128)S(1)}, f32[24,2304]{1,0:T(8,128)}, u32[]{:S(2)}) copy-start(f32[24,2304]{1,0:T(8,128)} %get-tuple-element.69) | copy-start | bytes 663556
  591.9 12.6 %copy-start.49 = (pred[24,2304]{1,0:T(8,128)(4,1)S(1)}, pred[24,2304]{1,0:T(8,128)(4,1)}, u32[]{:S(2)}) copy-start(pred[24,2304]{1,0:T(8,128)(4,1)} %and_and_fusion) | copy-start | bytes 165892
  600.0 17.3 %all-to-all-start.9 = ((bf16[4,2,55296]{2,1,0:T(2,128)(2,1)}), bf16[4,2,55296]{2,1,0:T(2,128)(2,1)}, u32[]{:S(2)}, u32[]{:S(2)}) async-start(bf16[4,2,55296]{2,1,0:T(2,128)(2,1)} %reshape.1350), calls=%async_computation.9 | async-start | bytes 1769472 | tf_op jit(solution)/shard_map/all_to_all | solution.py:120
  625.9 9.0 %copy-start.41 = (bf16[1,4,8,24]{3,2,1,0:T(8,128)(2,1)S(1)}, bf16[1,4,8,24]{3,2,1,0:T(8,128)(2,1)}, u32[]{:S(2)}) copy-start(bf16[1,4,8,24]{3,2,1,0:T(8,128)(2,1)} %copy-done.39) | copy-start | bytes 4612
  625.9 9.0 %copy-start.45 = (bf16[1,4,8,24]{3,2,1,0:T(8,128)(2,1)S(1)}, bf16[1,4,8,24]{3,2,1,0:T(8,128)(2,1)}, u32[]{:S(2)}) copy-start(bf16[1,4,8,24]{3,2,1,0:T(8,128)(2,1)} %copy-done.43) | copy-start | bytes 4612
  694.9 10.2 %copy-start.34 = (bf16[1,8,64,4,96]{4,2,3,1,0:T(8,128)(2,1)S(1)}, bf16[1,8,64,4,96]{4,2,3,1,0:T(8,128)(2,1)}, u32[]{:S(2)}) copy-start(bf16[1,8,64,4,96]{4,2,3,1,0:T(8,128)(2,1)} %get-tuple-element.70) | copy-start | bytes 1179652
  694.9 10.2 %copy-start.37 = (bf16[1,8,64,4,96]{4,2,3,1,0:T(8,128)(2,1)S(1)}, bf16[1,8,64,4,96]{4,2,3,1,0:T(8,128)(2,1)}, u32[]{:S(2)}) copy-start(bf16[1,8,64,4,96]{4,2,3,1,0:T(8,128)(2,1)} %get-tuple-element.71) | copy-start | bytes 1179652
  (38 other events, 120.1 us)
